TPU v7x, 32 devices: a whole 2x2x4 slice. The times are simulated.
32 devices in a mesh: pts: 4 (over y, x), med: 8 (over z, core).
Axes of the slice: x: 2, y: 2, z: 4, core: 2. Of those that a mesh axis runs over, the one named last changes fastest.
Arguments:
- points: float32 [65536, 1024], P(('pts', 'med')), may hold values from -6 to 6
- weights: float32 [65536], P(('pts', 'med')), may hold values from 0.2 to 6
- medoid_ids: int32 [512], replicated, may hold values from 0 to 65535, as said below
Outputs:
- cover: float32 [65536], P(('pts', 'med'))
- total: float32 [], replicated
Inputs may be any that keep to these rules, and one draw needn't show every extreme that they name: `medoid_ids`: distinct row numbers; the points of one device hold at most 24 medoids, and some device holds exactly 24 in every draw.
All inputs are finite; a program needn't handle non-finite values.
Results may differ from a plain program's by a relative error of at most 0.00005.
Values sent between devices are 32-bit elements; how exact they have to be, the bound alone decides.
A program may use at most 128 MiB of HBM per device.

v0:
```python
import jax
import jax.numpy as jnp
from jax import lax
from jax.sharding import PartitionSpec as P

MED_DEV = 16
EPS = 1e-06


def best_match(unit, block, offset):
    sims = lax.dot_general(
        unit,
        block,
        (((1,), (1,)), ((), ())),
        precision=lax.Precision.HIGHEST,
        preferred_element_type=jnp.float32,
    )
    return jnp.max(sims + offset[None, :], axis=1)


def slot_offsets(counts, global_rows, group_pts, group_med, capacity):
    group_rows = group_pts * capacity
    med_of = global_rows // group_rows
    within = global_rows % group_rows
    pts_of = within // capacity
    slot_of = within % capacity
    device_of = pts_of * group_med + med_of
    devices = jnp.arange(group_pts * group_med, dtype=jnp.int32)
    owned_count = jnp.sum(
        jnp.where(device_of[:, None] == devices[None, :], counts[None, :], 0), axis=1
    )
    return jnp.where(slot_of < owned_count, 0.0, -4.0).astype(jnp.float32)


def body(points, weights, medoid_ids):
    rows = points.shape[0]
    capacity = MED_DEV + MED_DEV // 2
    group_pts = lax.axis_size("pts")
    group_med = lax.axis_size("med")
    unit = points * lax.rsqrt(jnp.sum(points * points, axis=1, keepdims=True) + EPS)
    med_index = lax.axis_index("med")
    row_start = (lax.axis_index("pts") * group_med + med_index) * rows
    local = medoid_ids - row_start
    owned = jnp.logical_and(local >= 0, local < rows).astype(jnp.int32)
    rank = jnp.cumsum(owned) - 1
    slot_ids = jnp.arange(capacity, dtype=jnp.int32)
    select = jnp.logical_and(owned[None, :] == 1, rank[None, :] == slot_ids[:, None]).astype(
        jnp.int32
    )
    position = jnp.sum(select * local[None, :], axis=1)
    valid = jnp.sum(select, axis=1) > 0
    mine = jnp.take(unit, position, axis=0) * valid[:, None].astype(jnp.float32)
    owner_of = medoid_ids // rows
    devices = jnp.arange(group_pts * group_med, dtype=jnp.int32)
    counts = jnp.sum((owner_of[None, :] == devices[:, None]).astype(jnp.int32), axis=1)
    block = lax.all_gather(mine, "pts", axis=0, tiled=True)
    start_best = jnp.full((rows,), -8.0, jnp.float32)
    piece = lax.all_gather(block, "med", axis=0, tiled=True)
    global_rows = jnp.arange(piece.shape[0], dtype=jnp.int32)
    piece_offset = slot_offsets(counts, global_rows, group_pts, group_med, capacity)
    cover = jnp.maximum(start_best, best_match(unit, piece, piece_offset))
    both_sums = lax.psum(jnp.stack([jnp.sum(weights * cover), jnp.sum(weights)]), ("pts", "med"))
    return (cover, both_sums[0] / both_sums[1])


def solution(mesh):
    return jax.shard_map(
        body,
        mesh=mesh,
        in_specs=(P(("pts", "med"), None), P(("pts", "med")), P()),
        out_specs=(P(("pts", "med")), P()),
        check_vma=False,
    )
```

profile of v0, /device:TPU:0, one launch (start us, length us, event | category | flops | bytes accessed | tf_op | source)
XLA Modules:
  0.0 147.5 jit_solution(15723708422780872622)
XLA Ops:
  7.2 0.0 all-gather.2.cloned.1.call-start
  7.2 0.7 convert_compare_fusion
  7.9 0.3 reduce-window.9
  8.2 0.1 slice.13
  8.3 0.1 slice_reduce_fusion
  8.4 0.1 add_bitcast_fusion
  8.5 0.1 convert_reduce_fusion.1
  8.7 4.1 %multiply_reduce_fusion = f32[2048]{0:T(1024)S(1)} fusion(f32[2048,1024]{1,0:T(8,128)} %param.3), kind=kLoop, calls=%fused_computation.1 | loop fusion | flops 4192256 | bytes 8396800 | tf_op jit(solution)/shard_map/reduce_sum | solution.py:40
  12.9 1.2 copy-done
  14.1 3.8 %broadcast_multiply_fusion = f32[2048,1024]{1,0:T(8,128)} fusion(f32[2048,1024]{1,0:T(8,128)S(1)} %copy-done, f32[2048]{0:T(1024)S(1)} %add_rsqrt_fusion), kind=kLoop, calls=%fused_computation.3 | loop fusion | flops 2097152 | bytes 16785408 | tf_op jit(solution)/shard_map/mul | solution.py:40
  17.9 4.0 %gather_fusion = f32[24,1024]{1,0:T(8,128)S(1)} fusion(f32[2048,1024]{1,0:T(8,128)} %broadcast_multiply_fusion, s32[1024]{0:T(1024)S(1)} %pad_clamp_fusion), kind=kCustom, calls=%fused_computation | custom fusion | bytes 196704 | tf_op jit(solution)/shard_map/jit(_take)/gather | solution.py:52
  22.0 0.1 select_multiply_fusion
  22.0 11.7 %all_gather.6 = f32[96,1024]{1,0:T(8,128)} all-gather(f32[24,1024]{1,0:T(8,128)S(1)} %select_multiply_fusion), channel_id=1, replica_groups=mesh['pts'=4,'med'=8] {'pts'}, dimensions={0}, use_global_device_ids=true | all-gather | bytes 491520 | tf_op jit(solution)/shard_map/all_gather | solution.py:56
  33.7 0.0 all-gather.2.cloned.1.call-update
  33.8 0.0 copy-done.2
  33.8 0.1 convert_reduce_fusion
  33.9 0.1 select_reduce_fusion
  34.1 0.0 copy-start.1
  34.1 38.3 %all-gather.2.cloned.1.call-done = f32[768,1024]{1,0:T(8,128)} async-done(((f32[96,1024]{1,0:T(8,128)}), f32[768,1024]{1,0:T(8,128)}) %all-gather.2.cloned.1.call-update) | async-done | bytes 3145744 | tf_op jit(solution)/shard_map/all_gather | solution.py:58
  72.4 23.2 %add_reduce_fusion = f32[2048]{0:T(1024)S(1)} fusion(f32[2048,1024]{1,0:T(8,128)} %broadcast_multiply_fusion, f32[768,1024]{1,0:T(8,128)} %all-gather.2.cloned.1.call-done, f32[768]{0:T(1024)S(1)} %fusion.14), kind=kOutput, calls=%fused_computation.2 | convolution fusion | flops 19330496512 | bytes 11545600 | tf_op jit(solution)/shard_map/dot_general | solution.py:11
  95.7 1.3 multiply_reduce_fusion.1
  97.0 1.4 pad_maximum_fusion
  98.4 39.2 %psum.7 = f32[2]{0:T(128)S(1)} all-reduce(f32[2]{0:T(128)S(1)} %pad_maximum_fusion), channel_id=1, replica_groups=mesh['pts'=4,'med'=8] {'pts','med'}, use_global_device_ids=true, to_apply=%region_10.11 | all-reduce | flops 2 | bytes 16 | tf_op jit(solution)/shard_map/psum | solution.py:62
  137.5 0.6 fusion.18
  (12 shorter events, 0.1 us)
Async XLA Ops:
  7.2 65.2 %all-gather.2.cloned.1.call-start = ((), (), s32[]{:S(2)}) async-start(), calls=%async_computation | async-start | bytes 3538944 | tf_op jit(solution)/shard_map/all_gather | solution.py:58
  8.3 5.8 %copy-start = (f32[2048,1024]{1,0:T(8,128)S(1)}, f32[2048,1024]{1,0:T(8,128)}, u32[]{:S(2)}) copy-start(f32[2048,1024]{1,0:T(8,128)} %param.3) | copy-start | bytes 25165828
  14.1 19.7 %copy-start.2 = (s32[512]{0:T(512)S(1)}, s32[512]{0:T(512)}, u32[]{:S(2)}) copy-start(s32[512]{0:T(512)} %param.5) | copy-start | bytes 6148
  34.1 61.6 %copy-start.1 = (f32[2048]{0:T(1024)S(1)}, f32[2048]{0:T(1024)}, u32[]{:S(2)}) copy-start(f32[2048]{0:T(1024)} %param.4) | copy-start | bytes 24580
Sparse Core Ops, SparseCore 0:
  33.9 38.4 all-gather.1
where the time goes:
time: 148 us; the launch traced here: 147 us
  blocking collectives  50.9 us (34%)
  waiting for transfers between devices  38.4 us (26%)
  matrix products  23.2 us (16%)
  between operations  16.6 us (11%)
  other arithmetic  12.3 us (8%)
  local copies, waits for them, and re-layouts  6.06 us (4%)
    psum x1, blocking collectives, body(): lax.psum(jnp.stack([jnp.sum(weights * cover), jnp.sum(weights)]), ('pts',...  39.2 us
    all_gather x1, waiting for transfers between devices, body(): piece = lax.all_gather(block, 'med', axis=0, tiled=True)  38.3 us
    dot_general x1, matrix products, best_match(): lax.dot_general(unit, block, (((1,), (1,)), ((), ())), precision=lax.Prec...  23.2 us
    all_gather x1, blocking collectives, body(): block = lax.all_gather(mine, 'pts', axis=0, tiled=True)  11.7 us
    reduce_sum x1, other arithmetic, body(): jnp.sum(points * points, axis=1, keepdims=True) + EPS  4.15 us
    gather x1, local copies, waits for them, and re-layouts, body(): mine = jnp.take(unit, position, axis=0) * valid[:, None].astype(jnp.float32)  4.02 us
    mul x1, other arithmetic, body(): points * lax.rsqrt(jnp.sum(points * points, axis=1, keepdims=True) + EPS)  3.83 us
  transfers between devices with their start and end apart: 1, of which 1 were waited for; matrix products, arithmetic and copies ran while one was open for 0% of the time, Pallas kernels for 0%

commit v1 on v0

--- a/solution.py
+++ b/solution.py
@@ -59,7 +59,10 @@
     global_rows = jnp.arange(piece.shape[0], dtype=jnp.int32)
     piece_offset = slot_offsets(counts, global_rows, group_pts, group_med, capacity)
     cover = jnp.maximum(start_best, best_match(unit, piece, piece_offset))
-    both_sums = lax.psum(jnp.stack([jnp.sum(weights * cover), jnp.sum(weights)]), ("pts", "med"))
+    both_sums = jnp.sum(
+        lax.all_gather(jnp.stack([jnp.sum(weights * cover), jnp.sum(weights)]), ("pts", "med")),
+        axis=0,
+    )
     return (cover, both_sums[0] / both_sums[1])
 
 

time: 148 us -> 148 us (level)
    psum x1 -> x0, blocking collectives: 39.2 us -> none  [body(): lax.psum(jnp.stack([jnp.sum(weights * cover), jnp.sum(weights)]), ('pts',...]
    unnamed x0 -> x1, blocking collectives: none -> 39.2 us
    unnamed x0 -> x1, other arithmetic: none -> 1.5 us
where the time goes in v1:
time: 148 us
  blocking collectives  50.9 us (34%)
  waiting for transfers between devices  38.4 us (26%)
  matrix products  23.3 us (16%)
  between operations  16.7 us (11%)
  other arithmetic  12.4 us (8%)
  local copies, waits for them, and re-layouts  6.16 us (4%)
    unnamed x1, blocking collectives  39.2 us
    all_gather x1, waiting for transfers between devices, body(): piece = lax.all_gather(block, 'med', axis=0, tiled=True)  38.3 us
    dot_general x1, matrix products, best_match(): lax.dot_general(unit, block, (((1,), (1,)), ((), ())), precision=lax.Prec...  23.3 us
    all_gather x1, blocking collectives, body(): block = lax.all_gather(mine, 'pts', axis=0, tiled=True)  11.7 us
    reduce_sum x1, other arithmetic, body(): jnp.sum(points * points, axis=1, keepdims=True) + EPS  4.15 us
    gather x1, local copies, waits for them, and re-layouts, body(): mine = jnp.take(unit, position, axis=0) * valid[:, None].astype(jnp.float32)  4.02 us
    mul x1, other arithmetic, body(): points * lax.rsqrt(jnp.sum(points * points, axis=1, keepdims=True) + EPS)  3.83 us
  transfers between devices with their start and end apart: 1, of which 1 were waited for; matrix products, arithmetic and copies ran while one was open for 0% of the time, Pallas kernels for 0%

profile of v1, /device:TPU:0, one launch (start us, length us, event | category | flops | bytes accessed | tf_op | source)
XLA Modules:
  0.0 147.7 jit_solution(15266913729782118390)
XLA Ops:
  7.2 0.0 all-gather.3.cloned.1.call-start
  7.2 0.7 convert_compare_fusion
  7.9 0.3 reduce-window.9
  8.2 0.1 slice.13
  8.3 0.1 slice_reduce_fusion
  8.5 0.1 add_bitcast_fusion
  8.5 0.1 convert_reduce_fusion.1
  8.7 4.1 %multiply_reduce_fusion = f32[2048]{0:T(1024)S(1)} fusion(f32[2048,1024]{1,0:T(8,128)} %param.3), kind=kLoop, calls=%fused_computation.1 | loop fusion | flops 4192256 | bytes 8396800 | tf_op jit(solution)/shard_map/reduce_sum | solution.py:40
  12.9 1.2 copy-done
  14.1 3.8 %broadcast_multiply_fusion = f32[2048,1024]{1,0:T(8,128)} fusion(f32[2048,1024]{1,0:T(8,128)S(1)} %copy-done, f32[2048]{0:T(1024)S(1)} %add_rsqrt_fusion), kind=kLoop, calls=%fused_computation.3 | loop fusion | flops 2097152 | bytes 16785408 | tf_op jit(solution)/shard_map/mul | solution.py:40
  17.9 4.0 %gather_fusion = f32[24,1024]{1,0:T(8,128)S(1)} fusion(f32[2048,1024]{1,0:T(8,128)} %broadcast_multiply_fusion, s32[1024]{0:T(1024)S(1)} %pad_clamp_fusion), kind=kCustom, calls=%fused_computation | custom fusion | bytes 196704 | tf_op jit(solution)/shard_map/jit(_take)/gather | solution.py:52
  22.0 0.1 select_multiply_fusion
  22.0 11.7 %all_gather.12 = f32[96,1024]{1,0:T(8,128)} all-gather(f32[24,1024]{1,0:T(8,128)S(1)} %select_multiply_fusion), channel_id=1, replica_groups=mesh['pts'=4,'med'=8] {'pts'}, dimensions={0}, use_global_device_ids=true | all-gather | bytes 491520 | tf_op jit(solution)/shard_map/all_gather | solution.py:56
  33.8 0.0 all-gather.3.cloned.1.call-update
  33.8 0.1 convert_reduce_fusion
  34.0 0.1 select_reduce_fusion
  34.1 0.0 copy-start.1
  34.1 38.3 %all-gather.3.cloned.1.call-done = f32[768,1024]{1,0:T(8,128)} async-done(((f32[96,1024]{1,0:T(8,128)}), f32[768,1024]{1,0:T(8,128)}) %all-gather.3.cloned.1.call-update) | async-done | bytes 3145744 | tf_op jit(solution)/shard_map/all_gather | solution.py:58
  72.4 23.3 %add_reduce_fusion = f32[2048]{0:T(1024)S(1)} fusion(f32[2048,1024]{1,0:T(8,128)} %broadcast_multiply_fusion, f32[768,1024]{1,0:T(8,128)} %all-gather.3.cloned.1.call-done, f32[768]{0:T(1024)S(1)} %fusion.14), kind=kOutput, calls=%fused_computation.2 | convolution fusion | flops 19330496512 | bytes 11545600 | tf_op jit(solution)/shard_map/dot_general | solution.py:11
  95.7 1.3 multiply_reduce_fusion.1
  97.0 1.5 %maximum_dynamic-update-slice_fusion = f32[64]{0:T(128)S(1)} fusion(f32[64]{0:T(128)S(1)} %broadcast.176, u32[]{:T(128)S(6)} %multiply.1, f32[1]{0:T(128)} %bitcast.5, f32[1]{0:T(128)} %bitcast.4), kind=kLoop, calls=%fused_computation.57 | loop fusion | flops 2 | bytes 268
  98.5 39.2 %all-reduce = f32[64]{0:T(128)S(1)} all-reduce(f32[64]{0:T(128)S(1)} %maximum_dynamic-update-slice_fusion), channel_id=2, replica_groups=mesh['pts'=4,'med'=8] {'pts','med'}, use_global_device_ids=true, to_apply=%add | all-reduce | flops 64 | bytes 512
  137.6 0.1 reshape.121
  137.7 0.6 fusion.18
  (15 shorter events, 0.2 us)
Async XLA Ops:
  7.2 65.3 %all-gather.3.cloned.1.call-start = ((), (), s32[]{:S(2)}) async-start(), calls=%async_computation | async-start | bytes 3538944 | tf_op jit(solution)/shard_map/all_gather | solution.py:58
  8.3 5.8 %copy-start = (f32[2048,1024]{1,0:T(8,128)S(1)}, f32[2048,1024]{1,0:T(8,128)}, u32[]{:S(2)}) copy-start(f32[2048,1024]{1,0:T(8,128)} %param.3) | copy-start | bytes 25165828
  14.1 19.7 %copy-start.2 = (s32[512]{0:T(512)S(1)}, s32[512]{0:T(512)}, u32[]{:S(2)}) copy-start(s32[512]{0:T(512)} %param.5) | copy-start | bytes 6148
  34.1 61.6 %copy-start.1 = (f32[2048]{0:T(1024)S(1)}, f32[2048]{0:T(1024)}, u32[]{:S(2)}) copy-start(f32[2048]{0:T(1024)} %param.4) | copy-start | bytes 24580
Sparse Core Ops, SparseCore 0:
  33.9 38.4 all-gather.2
